TPU v7x, 16 devices: a whole 2x2x2 slice. The times are simulated.
16 devices in a mesh: dp: 4 (over z, y), tp: 4 (over x, core).
Axes of the slice: x: 2, y: 2, z: 2, core: 2. Of those that a mesh axis runs over, the one named last changes fastest.
Arguments:
- hidden: bfloat16 [128, 3072], P('dp'), parts along dimension 0
- final_gain: bfloat16 [3072], replicated
- embed_table: bfloat16 [128256, 3072], P(None, 'tp')
- targets: int32 [128], P('dp'), parts along dimension 0
- temperature: float32 [], replicated
Outputs:
- output 1: float32 [128], P('dp'), parts along dimension 0
- output 2: float32 [128], P('dp'), parts along dimension 0
- output 3: bfloat16 [128, 128256], P('dp', 'tp'), parts along dimension 0
There are 4 independent parts. A program takes and returns all parts, laid end to end along the dimension named above; an argument that names none is the same for every part.
All inputs are finite; a program needn't handle non-finite values.
Results may differ from a plain program's by a relative error of at most 0.001.
Values sent between devices are 32-bit elements.
A program may use at most 1 GiB of HBM per device.

v0:
```python
import jax
import jax.numpy as jnp
from jax import lax
from jax.sharding import PartitionSpec as P

NORM_EPS = 1e-6


def solution(mesh):
    def local_scores(hidden, final_gain, table_cols, targets, value_a11):
        shard_index = lax.axis_index('tp')
        col_width = table_cols.shape[1]
        col_start = shard_index * col_width
        hidden_f32 = hidden.astype(jnp.float32)
        inv_rms = lax.rsqrt(jnp.mean(hidden_f32 * hidden_f32, axis=-1, keepdims=True) + NORM_EPS)
        hidden_cols = lax.dynamic_slice_in_dim(hidden, col_start, col_width, axis=1).astype(jnp.float32)
        gain_cols = lax.dynamic_slice_in_dim(final_gain, col_start, col_width).astype(jnp.float32)
        normed_cols = (hidden_cols * inv_rms * gain_cols).astype(jnp.bfloat16)
        partial_logits = lax.dot_general(normed_cols, table_cols, (((1,), (1,)), ((), ())),
                                         preferred_element_type=jnp.float32)
        logits = lax.psum_scatter(partial_logits, 'tp', scatter_dimension=1, tiled=True) / value_a11
        row_max = lax.pmax(jnp.max(logits, axis=-1), 'tp')
        shard_sum = jnp.sum(jnp.exp(logits - row_max[:, None]), axis=-1)
        log_norm = row_max + jnp.log(lax.psum(shard_sum, 'tp'))
        target_rows = jnp.take(table_cols, targets, axis=0)
        target_part = jnp.einsum('nd,nd->n', normed_cols, target_rows,
                                 preferred_element_type=jnp.float32)
        target_logit = lax.psum(target_part, 'tp') / value_a11
        token_probs = jnp.exp(logits - log_norm[:, None]).astype(jnp.bfloat16)
        return log_norm, target_logit - log_norm, token_probs

    return jax.shard_map(local_scores, mesh=mesh,
                         in_specs=(P('dp', None), P(None), P(None, 'tp'), P('dp'), P()),
                         out_specs=(P('dp'), P('dp'), P('dp', 'tp')),
                         check_vma=False)
```

profile of v0, /device:TPU:0, one launch (start us, length us, event | category | flops | bytes accessed | tf_op | source)
XLA Modules:
  0.0 578.6 jit_solution(5852095222621335674)
XLA Ops:
  7.2 0.0 reduce-scatter.4.cloned.1.call-start
  7.2 1.1 multiply_reduce_fusion
  8.3 0.8 dynamic-slice_convert_fusion
  9.1 90.9 %convolution_bitcast_fusion = f32[128256,32]{1,0:T(8,128)} fusion(bf16[128256,768]{1,0:T(8,128)(2,1)} %param.7, f32[768]{0:T(1024)S(1)} %dynamic-slice_convert_fusion, f32[32]{0:T(128)S(1)} %add_rsqrt_fusion, bf16[32,3072]{1,0:T(8,128)(2,1)} %param.5, s32[]{:T(128)S(6)} %select_n.13), kind=kOutput, calls=%fused_computation.1 | convolution fusion | flops 6304137216 | bytes 213470336
  100.0 0.0 copy-start.1
  100.0 0.0 reduce-scatter.4.cloned.1.call-update
  100.7 0.0 copy-done.1
  100.7 1.5 gather_fusion
  102.2 1.0 fusion
  103.2 435.5 %reduce-scatter.4.cloned.1.call-done = f32[32064,32]{1,0:T(8,128)} async-done(((f32[128256,32]{1,0:T(8,128)}), f32[32064,32]{1,0:T(8,128)}) %reduce-scatter.4.cloned.1.call-update) | async-done | bytes 4104208
  538.7 11.4 %copy.14 = f32[32,32064]{1,0:T(8,128)} copy(f32[32,32064]{0,1:T(8,128)} %bitcast.6) | data formatting | bytes 8208384
  550.2 2.5 fusion.2
  552.7 5.8 pmax.7
  558.5 3.0 exponential_reduce_fusion
  561.5 5.7 all-reduce
  567.1 0.5 divide_subtract_fusion
  567.6 0.0 copy-start
  567.6 4.1 exponential_convert_fusion
  571.8 0.0 copy-done
  (4 shorter events, 0.0 us)
Async XLA Ops:
  7.2 531.6 %reduce-scatter.4.cloned.1.call-start = ((), (), s32[]{:S(2)}) async-start(), calls=%async_computation.1 | async-start | bytes 82083840
  100.0 0.7 copy-start.1
  567.6 4.1 copy-start
Sparse Core Ops, SparseCore 0:
  100.1 438.5 reduce-scatter.3
where the time goes:
time: 579 us
  waiting for transfers between devices  436 us (75%)
  matrix products  90.9 us (16%)
  between operations  14.7 us (3%)
  other arithmetic  13 us (2%)
  local copies, waits for them, and re-layouts  13 us (2%)
  blocking collectives  11.4 us (2%)
    unnamed x2, waiting for transfers between devices  436 us
    unnamed x1, matrix products  90.9 us
  transfers between devices with their start and end apart: 1, of which 1 were waited for; matrix products, arithmetic and copies ran while one was open for 0% of the time, Pallas kernels for 0%

commit v1 on v0

v1 whole, which is shorter than its diff:
```python
import functools

import jax
import jax.numpy as jnp
from jax import lax
from jax.experimental import pallas as pl
from jax.experimental.pallas import tpu as pltpu
from jax.sharding import PartitionSpec as P

NORM_EPS = 1e-6
MESH = pl.DeviceIdType.MESH
F32 = jnp.float32
BF16 = jnp.bfloat16
G = 4
R = 256
NBUF = 8


def scores_kernel(dims, temp_ref, tgt_ref, hid_hbm, gain_hbm, table, logits_ref, stats_ref, lncol_ref,
                  hid, gain, w, ring, tail, ps, po, ls, lo, ra, rb, rx, acc, st,
                  in_sem, ring_sem, tail_sem, as_sem, ar_sem, bs_sem, br_sem, xs_sem, xr_sem, ss_sem, sr_sem):
    tokens, hidden_size, width, vq, nf, rt = dims
    me = lax.axis_index('tp')
    x = me // 2
    c = me % 2
    sib = 2 * x + (1 - c)
    xpeer = 2 * (1 - x) + c
    diag = 2 * (1 - x) + (1 - c)
    rows = G * R
    trows = G * rt
    last = nf * R
    steps = 4 * nf

    def table_copy(s):
        phase = s // (2 * nf)
        j = s - phase * (2 * nf)
        k = j // 2
        which = j - 2 * k
        xx = (1 - phase) * (1 - x) + phase * x
        cc = (1 - which) * (1 - c) + which * c
        start = pl.multiple_of((2 * xx + cc) * vq + k * rows, 64)
        slot = s % NBUF
        return pltpu.make_async_copy(table.at[pl.ds(start, rows)], ring.at[slot], ring_sem.at[slot])

    def tail_copy(i):
        xx = (1 - x) if i < 2 else x
        cc = (1 - c) if i % 2 == 0 else c
        start = pl.multiple_of((2 * xx + cc) * vq + nf * rows, 64)
        return pltpu.make_async_copy(table.at[pl.ds(start, trows)], tail.at[i], tail_sem.at[i])

    def chunk(k):
        return pl.ds(pl.multiple_of(k * R, R), R)

    tail_rows = pl.ds(last, rt)

    def remote(src, dst, send, recv, k, sl, dev):
        return pltpu.make_async_remote_copy(src_ref=src.at[sl], dst_ref=dst.at[sl], send_sem=send.at[k],
                                            recv_sem=recv.at[k], device_id={'tp': dev}, device_id_type=MESH)

    def a_copy(k, sl):
        return remote(ps, ra, as_sem, ar_sem, k, sl, sib)

    def b_copy(k, sl):
        return remote(ls, rb, bs_sem, br_sem, k, sl, sib)

    def x_copy(k, sl):
        return remote(po, rx, xs_sem, xr_sem, k, sl, xpeer)

    hid_copy = pltpu.make_async_copy(hid_hbm, hid, in_sem.at[0])
    gain_copy = pltpu.make_async_copy(gain_hbm, gain, in_sem.at[1])
    hid_copy.start()
    gain_copy.start()
    for s in range(NBUF):
        table_copy(s).start()
    for i in range(4):
        tail_copy(i).start()

    barrier = pltpu.get_barrier_semaphore()
    for peer in (sib, xpeer, diag):
        pl.semaphore_signal(barrier, inc=1, device_id={'tp': peer}, device_id_type=MESH)

    hid_copy.wait()
    gain_copy.wait()
    hf = hid[...].astype(F32)
    inv = lax.rsqrt(jnp.mean(hf * hf, axis=-1, keepdims=True) + NORM_EPS)
    cols = pl.ds(pl.multiple_of(me * width, 128), width)
    u = (hid[:, cols].astype(F32) * inv * gain[:, cols].astype(F32)).astype(BF16).astype(F32)
    u_t = jnp.concatenate([u] * G, axis=0).T
    group = lax.broadcasted_iota(jnp.int32, (width, 128), 1) // tokens
    for g in range(G):
        w[g * width:(g + 1) * width, :] = jnp.where(group == g, u_t, 0.0).astype(BF16)
    acc[0] = jnp.full((8, 128), -jnp.inf, F32)
    acc[1] = jnp.zeros((8, 128), F32)
    acc[2] = jnp.zeros((8, 128), F32)
    pl.semaphore_wait(barrier, 3)

    def packed_dot(view, n):
        total = None
        for g in range(G):
            part = jnp.dot(view[g * n:(g + 1) * n, :], w[g * width:(g + 1) * width, :], preferred_element_type=F32)
            total = part if total is None else total + part
        return total

    def ring_dot(s, dst, sl):
        table_copy(s).wait()
        dst[sl, :] = packed_dot(ring.at[s % NBUF], R)

        @pl.when(s + NBUF < steps)
        def _():
            table_copy(s + NBUF).start()

    def add_sibling(k, sl):
        a_copy(k, sl).wait_recv()
        po[sl, :] = po[sl, :] + ra[sl, :]

    @pl.loop(0, nf)
    def _(k):
        ring_dot(2 * k, ps, chunk(k))

        @pl.when(k > 0)
        def _():
            add_sibling(k - 1, chunk(k - 1))

        a_copy(k, chunk(k)).start()
        ring_dot(2 * k + 1, po, chunk(k))

        @pl.when(k > 0)
        def _():
            x_copy(k - 1, chunk(k - 1)).start()

    tail_copy(0).wait()
    ps[tail_rows, :] = packed_dot(tail.at[0], rt)
    add_sibling(nf - 1, chunk(nf - 1))
    a_copy(nf, tail_rows).start()
    tail_copy(1).wait()
    po[tail_rows, :] = packed_dot(tail.at[1], rt)
    x_copy(nf - 1, chunk(nf - 1)).start()

    @pl.loop(0, nf)
    def _(k):
        ring_dot(2 * nf + 2 * k, ls, chunk(k))

        @pl.when(k == 0)
        def _():
            add_sibling(nf, tail_rows)

        ring_dot(2 * nf + 2 * k + 1, lo, chunk(k))

        @pl.when(k == 0)
        def _():
            x_copy(nf, tail_rows).start()

        b_copy(k, chunk(k)).start()

    tail_copy(2).wait()
    ls[tail_rows, :] = packed_dot(tail.at[2], rt)
    tail_copy(3).wait()
    lo[tail_rows, :] = packed_dot(tail.at[3], rt)
    b_copy(nf, tail_rows).start()

    temp = temp_ref[0, 0]
    lane_group = lax.broadcasted_iota(jnp.int32, (1, 128), 1) // tokens
    tgt = tgt_ref[...] - me * vq

    def logits_of(k, sl):
        b_copy(k, sl).wait_recv()
        x_copy(k, sl).wait_recv()
        return (lo[sl, :] + rb[sl, :] + rx[sl, :]) / temp

    def update(t, n, base):
        t3 = t.reshape(n // 8, 8, 128)
        m_old = acc[0]
        m_new = jnp.maximum(m_old, jnp.max(t3, axis=0))
        acc[0] = m_new
        acc[1] = acc[1] * jnp.exp(m_old - m_new) + jnp.sum(jnp.exp(t3 - m_new), axis=0)
        row = lax.broadcasted_iota(jnp.int32, (n, 128), 0)
        hit = row == (tgt - base - lane_group * n)
        acc[2] += jnp.sum(jnp.where(hit, t, 0.0).reshape(n // 8, 8, 128), axis=0)

    @pl.loop(0, nf)
    def _(k):
        t = logits_of(k, chunk(k))
        update(t, R, k * rows)
        tt = t.T
        for g in range(G):
            logits_ref[:, pl.ds(pl.multiple_of(k * rows + g * R, 128), R)] = tt[g * tokens:(g + 1) * tokens, :]

    t = logits_of(nf, tail_rows)
    update(t, rt, nf * rows)

    m = jnp.max(acc[0], axis=0, keepdims=True)
    for shift in (32, 64):
        m = jnp.maximum(m, pltpu.roll(m, shift, 1))
    total = jnp.sum(acc[1] * jnp.exp(acc[0] - m), axis=0, keepdims=True)
    hit = jnp.sum(acc[2], axis=0, keepdims=True)
    for shift in (32, 64):
        total = total + pltpu.roll(total, shift, 1)
        hit = hit + pltpu.roll(hit, shift, 1)
    st[me] = jnp.concatenate([m, total, hit, jnp.zeros((5, 128), F32)], axis=0)

    tt = jnp.concatenate([t, jnp.zeros((128 - rt, 128), F32)], axis=0).T
    parts = [tt[g * tokens:(g + 1) * tokens, :] for g in range(G)]
    lane = lax.broadcasted_iota(jnp.int32, (tokens, 128), 1)
    for i in range((G * rt + 127) // 128):
        tile = jnp.zeros((tokens, 128), F32)
        for g in range(G):
            off = g * rt - i * 128
            if off <= -rt or off >= 128:
                continue
            moved = pltpu.roll(parts[g], off % 128, 1) if off % 128 else parts[g]
            tile = jnp.where((lane >= off) & (lane < off + rt), moved, tile)
        logits_ref[:, nf * rows + i * 128:nf * rows + (i + 1) * 128] = tile

    stat_copies = []
    for i, peer in enumerate((sib, xpeer, diag)):
        copy = pltpu.make_async_remote_copy(src_ref=st.at[me], dst_ref=st.at[me], send_sem=ss_sem.at[i],
                                            recv_sem=sr_sem.at[i], device_id={'tp': peer}, device_id_type=MESH)
        copy.start()
        stat_copies.append(copy)
    for copy in stat_copies:
        copy.wait_recv()
    ms = [st[i, 0:1, :] for i in range(4)]
    top = jnp.maximum(jnp.maximum(ms[0], ms[1]), jnp.maximum(ms[2], ms[3]))
    norm = jnp.zeros((1, 128), F32)
    hit = jnp.zeros((1, 128), F32)
    for i in range(4):
        norm = norm + st[i, 1:2, :] * jnp.exp(ms[i] - top)
        hit = hit + st[i, 2:3, :]
    log_norm = top + jnp.log(norm)
    stats_ref[...] = jnp.concatenate([log_norm, hit - log_norm, jnp.zeros((6, 128), F32)], axis=0)
    lncol_ref[...] = jnp.broadcast_to(log_norm, (128, 128)).T[:tokens, :]

    for copy in stat_copies:
        copy.wait_send()

    @pl.loop(0, nf)
    def _(k):
        a_copy(k, chunk(k)).wait_send()
        b_copy(k, chunk(k)).wait_send()
        x_copy(k, chunk(k)).wait_send()

    a_copy(nf, tail_rows).wait_send()
    b_copy(nf, tail_rows).wait_send()
    x_copy(nf, tail_rows).wait_send()


def probs_kernel(logits_ref, stats_ref, lncol_ref, ln_ref, tl_ref, probs_ref):
    @pl.when(pl.program_id(0) == 0)
    def _():
        ln_ref[...] = stats_ref[0:1, :32]
        tl_ref[...] = stats_ref[1:2, :32]

    probs_ref[...] = jnp.exp(logits_ref[...] - lncol_ref[:, 0:1]).astype(BF16)


def solution(mesh):
    def local_scores(hidden, final_gain, table, targets, temperature):
        tokens, hidden_size = hidden.shape
        vocab, width = table.shape
        vq = vocab // 4
        nf = vq // (G * R)
        rt = (vq - nf * G * R) // G
        packed = vq // G
        lanes = (vq + 127) // 128 * 128
        dims = (tokens, hidden_size, width, vq, nf, rt)
        tgt = jnp.tile(targets, G).reshape(1, G * tokens)
        vmem = pl.BlockSpec(memory_space=pltpu.VMEM)
        anyspace = pl.BlockSpec(memory_space=pl.ANY)
        nsem = nf + 1
        logits, stats, lncol = pl.pallas_call(
            functools.partial(scores_kernel, dims),
            out_shape=(jax.ShapeDtypeStruct((tokens, lanes), F32),
                       jax.ShapeDtypeStruct((8, 128), F32),
                       jax.ShapeDtypeStruct((tokens, 128), F32)),
            in_specs=[pl.BlockSpec(memory_space=pltpu.SMEM), vmem, anyspace, anyspace, anyspace],
            out_specs=(vmem, vmem, vmem),
            scratch_shapes=[
                pltpu.VMEM((tokens, hidden_size), BF16),
                pltpu.VMEM((1, hidden_size), BF16),
                pltpu.VMEM((G * width, 128), BF16),
                pltpu.VMEM((NBUF, G * R, width), BF16),
                pltpu.VMEM((4, G * rt, width), BF16),
            ] + [pltpu.VMEM((packed, 128), F32)] * 7 + [
                pltpu.VMEM((3, 8, 128), F32),
                pltpu.VMEM((4, 8, 128), F32),
                pltpu.SemaphoreType.DMA((2,)),
                pltpu.SemaphoreType.DMA((NBUF,)),
                pltpu.SemaphoreType.DMA((4,)),
            ] + [pltpu.SemaphoreType.DMA((nsem,))] * 6 + [
                pltpu.SemaphoreType.DMA((3,)),
                pltpu.SemaphoreType.DMA((3,)),
            ],
            compiler_params=pltpu.CompilerParams(collective_id=0, has_side_effects=True,
                                                 vmem_limit_bytes=56 * 2 ** 20),
        )(temperature.reshape(1, 1), tgt, hidden, final_gain.reshape(1, hidden_size), table)
        block = 8192
        log_norm, target_logprob, probs = pl.pallas_call(
            probs_kernel,
            grid=(pl.cdiv(vq, block),),
            out_shape=(jax.ShapeDtypeStruct((1, tokens), F32),
                       jax.ShapeDtypeStruct((1, tokens), F32),
                       jax.ShapeDtypeStruct((tokens, vq), BF16)),
            in_specs=[pl.BlockSpec((tokens, block), lambda i: (0, i)),
                      pl.BlockSpec((8, 128), lambda i: (0, 0)),
                      pl.BlockSpec((tokens, 128), lambda i: (0, 0))],
            out_specs=(pl.BlockSpec((1, tokens), lambda i: (0, 0)),
                       pl.BlockSpec((1, tokens), lambda i: (0, 0)),
                       pl.BlockSpec((tokens, block), lambda i: (0, i))),
        )(logits, stats, lncol)
        return log_norm.reshape(tokens), target_logprob.reshape(tokens), probs

    return jax.shard_map(local_scores, mesh=mesh,
                         in_specs=(P('dp', None), P(None), P(None, 'tp'), P('dp'), P()),
                         out_specs=(P('dp'), P('dp'), P('dp', 'tp')),
                         check_vma=False)
```

time: 579 us -> 114 us (0.20)
  waiting for transfers between devices: 436 us -> 0 us
  Pallas kernels: 0 us -> 110 us
  matrix products: 90.9 us -> 0 us
  between operations: 14.7 us -> 1.29 us
  other arithmetic: 13 us -> 0 us
  blocking collectives: 11.4 us -> 0 us
  local copies, waits for them, and re-layouts: 13 us -> 2.55 us
    unnamed x2 -> x0, waiting for transfers between devices: 436 us -> none
    pallas_call x0 -> x2, Pallas kernels: none -> 110 us  [the longest x1 106 us: local_scores(): pl.pallas_call(functools.partial(scores_kernel, dims), out_shape=(jax.Sha...]
    unnamed x1 -> x0, matrix products: 90.9 us -> none
    unnamed x5 -> x0, local copies, waits for them, and re-layouts: 11.4 us -> none
  transfers between devices with their start and end apart: 1 -> 0, of which waited for: 1 -> 0; matrix products, arithmetic and copies ran while one was open for 0% -> 0% of each run, Pallas kernels for 0% -> 0%
where the time goes in v1:
time: 114 us
  Pallas kernels  110 us (96%)
  local copies, waits for them, and re-layouts  2.55 us (2%)
  between operations  1.29 us (1%)
    pallas_call x1, Pallas kernels, local_scores(): pl.pallas_call(functools.partial(scores_kernel, dims), out_shape=(jax.Sha...  106 us
    pallas_call x1, Pallas kernels, local_scores(): pl.pallas_call(probs_kernel, grid=(pl.cdiv(vq, block),), out_shape=(jax.S...  4.55 us

profile of v1, /device:TPU:0, one launch (start us, length us, event | category | flops | bytes accessed | tf_op | source)
XLA Modules:
  0.0 114.1 jit_solution(13435640456364596633)
XLA Ops:
  1.3 0.7 tile.2
  1.9 0.6 reshape_tile.3.tgt_ref
  2.5 1.3 %reshape.20.gain_hbm = bf16[1,3072]{1,0:T(2,128)(2,1)} reshape(bf16[3072]{0:T(1024)(128)(2,1)} %param.6) | data formatting | bytes 12288 | tf_op jit(solution)/shard_map/reshape | solution.py:295
  3.8 105.7 %shard_map.76 = (f32[32,32128]{1,0:T(8,128)}, f32[8,128]{1,0:T(8,128)}, f32[32,128]{1,0:T(8,128)}) custom-call(f32[1,1]{1,0:T(1,128)} %bitcast.3.temp_ref, s32[1,128]{1,0:T(1,128)} %reshape_tile.3.tgt_ref, bf16[32,3072]{1,0:T(8,128)(2,1)} %hid_hbm.1, bf16[1,3072]{1,0:T(2,128)(2,1)} %reshape.20.gain_hbm, bf16[128256,768]{1,0:T(8,128)(2,1)} %table.1), custom_call_target="tpu_custom_call" | custom-call | tf_op jit(solution)/shard_map/pallas_call | solution.py:270
  109.5 4.5 %shard_map.77 = (f32[1,32]{1,0:T(1,128)}, f32[1,32]{1,0:T(1,128)}, bf16[32,32064]{1,0:T(8,128)(2,1)}) custom-call(f32[32,32128]{1,0:T(8,128)} %get-tuple-element.9.logits_ref, f32[8,128]{1,0:T(8,128)} %get-tuple-element.10.stats_ref, f32[32,128]{1,0:T(8,128)} %get-tuple-element.11.lncol_ref), custom_call_target="tpu_custom_call" | custom-call | tf_op jit(solution)/shard_map/pallas_call | solution.py:297

commit v2 on v1

v2 whole, which is shorter than its diff:
```python
import functools

import jax
import jax.numpy as jnp
from jax import lax
from jax.experimental import pallas as pl
from jax.experimental.pallas import tpu as pltpu
from jax.sharding import PartitionSpec as P

NORM_EPS = 1e-6
MESH = pl.DeviceIdType.MESH
F32 = jnp.float32
BF16 = jnp.bfloat16
G = 4
R = 256
NBUF = 8
PIECES = 2


def scores_kernel(dims, temp_ref, tgt_hbm, hid_hbm, gain_hbm, table, logits_ref, stats_ref, lncol_ref,
                  tgt_ref, hid, gain, gain32, w, ring, tail, ps, po, ls, lo, ra, rb, rx, st,
                  in_sem, ring_sem, tail_sem, as_sem, ar_sem, bs_sem, br_sem, xs_sem, xr_sem, ss_sem, sr_sem):
    tokens, hidden_size, width, vq, nf, rt = dims
    me = lax.axis_index('tp')
    x = me // 2
    c = me % 2
    sib = 2 * x + (1 - c)
    xpeer = 2 * (1 - x) + c
    diag = 2 * (1 - x) + (1 - c)
    rows = G * R
    trows = G * rt
    last = nf - 1
    steps = 4 * nf

    def table_copy(s):
        phase = s // (2 * nf)
        j = s - phase * (2 * nf)
        k = j // 2
        which = j - 2 * k
        xx = (1 - phase) * (1 - x) + phase * x
        cc = (1 - which) * (1 - c) + which * c
        start = pl.multiple_of((2 * xx + cc) * vq + k * rows, 64)
        slot = s % NBUF
        return pltpu.make_async_copy(table.at[pl.ds(start, rows)], ring.at[slot], ring_sem.at[slot])

    def tail_copy(i):
        xx = (1 - x) if i < 2 else x
        cc = (1 - c) if i % 2 == 0 else c
        start = pl.multiple_of((2 * xx + cc) * vq + nf * rows, 64)
        return pltpu.make_async_copy(table.at[pl.ds(start, trows)], tail.at[i], tail_sem.at[i])

    def chunk(k):
        return pl.ds(pl.multiple_of(k * R, R), R)

    tail_rows = pl.ds(nf * R, rt)

    def remote(src, dst, send, recv, k, sl, dev):
        return pltpu.make_async_remote_copy(src_ref=src.at[sl], dst_ref=dst.at[sl], send_sem=send.at[k],
                                            recv_sem=recv.at[k], device_id={'tp': dev}, device_id_type=MESH)

    def a_copy(k, sl):
        return remote(ps, ra, as_sem, ar_sem, k, sl, sib)

    def b_copy(k, sl):
        return remote(ls, rb, bs_sem, br_sem, k, sl, sib)

    def x_copy(k, sl):
        return remote(po, rx, xs_sem, xr_sem, k, sl, xpeer)

    piece = R // PIECES

    def x_piece(p):
        return x_copy(last if p == 0 else nf + p, pl.ds(last * R + p * piece, piece))

    hid_copy = pltpu.make_async_copy(hid_hbm, hid, in_sem.at[0])
    gain_copy = pltpu.make_async_copy(gain_hbm, gain, in_sem.at[1])
    tgt_copy = pltpu.make_async_copy(tgt_hbm, tgt_ref, in_sem.at[2])
    hid_copy.start()
    gain_copy.start()
    tail_copy(0).start()
    tail_copy(1).start()
    for s in range(NBUF):
        table_copy(s).start()
    tgt_copy.start()
    tail_copy(2).start()
    tail_copy(3).start()

    barrier = pltpu.get_barrier_semaphore()
    for peer in (sib, xpeer, diag):
        pl.semaphore_signal(barrier, inc=1, device_id={'tp': peer}, device_id_type=MESH)

    hid_copy.wait()
    gain_copy.wait()
    hf = hid[...].astype(F32)
    inv = lax.rsqrt(jnp.mean(hf * hf, axis=-1, keepdims=True) + NORM_EPS)
    cols = pl.ds(pl.multiple_of(me * width, 128), width)
    gain32[...] = gain[...].astype(F32)
    scaled = hid[:, cols].astype(F32) * inv
    u = jnp.concatenate([scaled[:, j * 128:(j + 1) * 128] * gain32[pl.ds(me * (width // 128) + j, 1), :]
                         for j in range(width // 128)], axis=1).astype(BF16).astype(F32)
    u_t = jnp.concatenate([u] * G, axis=0).T
    group = lax.broadcasted_iota(jnp.int32, (width, 128), 1) // tokens
    for g in range(G):
        w[g * width:(g + 1) * width, :] = jnp.where(group == g, u_t, 0.0).astype(BF16)
    pl.semaphore_wait(barrier, 3)

    def packed_dot(view, n):
        total = None
        for g in range(G):
            part = jnp.dot(view[g * n:(g + 1) * n, :], w[g * width:(g + 1) * width, :], preferred_element_type=F32)
            total = part if total is None else total + part
        return total

    def ring_dot(s, dst, sl):
        table_copy(s).wait()
        dst[sl, :] = packed_dot(ring.at[s % NBUF], R)

        @pl.when(s + NBUF < steps)
        def _():
            table_copy(s + NBUF).start()

    def add_sibling(k, sl):
        a_copy(k, sl).wait_recv()
        po[sl, :] = po[sl, :] + ra[sl, :]

    tail_copy(0).wait()
    ps[tail_rows, :] = packed_dot(tail.at[0], rt)
    a_copy(nf, tail_rows).start()
    tail_copy(1).wait()
    po[tail_rows, :] = packed_dot(tail.at[1], rt)

    @pl.loop(0, nf)
    def _(k):
        ring_dot(2 * k, ps, chunk(k))
        a_copy(k, chunk(k)).start()

        @pl.when(k == 0)
        def _():
            add_sibling(nf, tail_rows)
            x_copy(nf, tail_rows).start()

        @pl.when(k > 0)
        def _():
            add_sibling(k - 1, chunk(k - 1))

        @pl.when(k == 1)
        def _():
            x_copy(k - 1, chunk(k - 1)).start()

        ring_dot(2 * k + 1, po, chunk(k))

        @pl.when(k > 1)
        def _():
            x_copy(k - 1, chunk(k - 1)).start()

    acc = st.at[me]
    acc[0] = jnp.full((8, 128), -jnp.inf, F32)
    acc[1] = jnp.zeros((8, 128), F32)
    acc[2] = jnp.zeros((8, 128), F32)
    tail_copy(2).wait()
    ls[tail_rows, :] = packed_dot(tail.at[2], rt)
    tail_copy(3).wait()
    lo[tail_rows, :] = packed_dot(tail.at[3], rt)
    add_sibling(last, chunk(last))

    @pl.loop(0, nf)
    def _(k):
        ring_dot(2 * nf + 2 * k, ls, chunk(k))

        @pl.when(k == 0)
        def _():
            b_copy(nf, tail_rows).start()
            for p in range(PIECES):
                x_piece(p).start()

        ring_dot(2 * nf + 2 * k + 1, lo, chunk(k))
        b_copy(k, chunk(k)).start()

    tgt_copy.wait()
    temp = temp_ref[0, 0]
    lane_group = lax.broadcasted_iota(jnp.int32, (1, 128), 1) // tokens
    tgt = jnp.concatenate([tgt_ref[...]] * G, axis=1) - me * vq

    def update(sl, n, base, stride):
        t = (lo[sl, :] + rb[sl, :] + rx[sl, :]) / temp
        t3 = t.reshape(n // 8, 8, 128)
        m_old = acc[0]
        m_new = jnp.maximum(m_old, jnp.max(t3, axis=0))
        acc[0] = m_new
        acc[1] = acc[1] * jnp.exp(m_old - m_new) + jnp.sum(jnp.exp(t3 - m_new), axis=0)
        row = lax.broadcasted_iota(jnp.int32, (n, 128), 0)
        hit = row == (tgt - base - lane_group * stride)
        acc[2] += jnp.sum(jnp.where(hit, t, 0.0).reshape(n // 8, 8, 128), axis=0)
        return t

    def put(t, n, base, stride):
        tt = t.T
        for g in range(G):
            logits_ref[:, pl.ds(pl.multiple_of(base + g * stride, 128), n)] = tt[g * tokens:(g + 1) * tokens, :]

    b_copy(nf, tail_rows).wait_recv()
    x_copy(nf, tail_rows).wait_recv()
    t = update(tail_rows, rt, nf * rows, rt)
    tt = jnp.concatenate([t, jnp.zeros((128 - rt, 128), F32)], axis=0).T
    parts = [tt[g * tokens:(g + 1) * tokens, :] for g in range(G)]
    lane = lax.broadcasted_iota(jnp.int32, (tokens, 128), 1)
    for i in range((G * rt + 127) // 128):
        tile = jnp.zeros((tokens, 128), F32)
        for g in range(G):
            off = g * rt - i * 128
            if off <= -rt or off >= 128:
                continue
            moved = pltpu.roll(parts[g], off % 128, 1) if off % 128 else parts[g]
            tile = jnp.where((lane >= off) & (lane < off + rt), moved, tile)
        logits_ref[:, nf * rows + i * 128:nf * rows + (i + 1) * 128] = tile

    @pl.loop(0, last)
    def _(k):
        b_copy(k, chunk(k)).wait_recv()
        x_copy(k, chunk(k)).wait_recv()
        put(update(chunk(k), R, k * rows, R), R, k * rows, R)

    b_copy(last, chunk(last)).wait_recv()
    for p in range(PIECES):
        x_piece(p).wait_recv()
        t = update(pl.ds(last * R + p * piece, piece), piece, last * rows + p * piece, R)
        put(t, piece, last * rows + p * piece, R)

    stat_copies = []
    for i, peer in enumerate((sib, xpeer, diag)):
        copy = pltpu.make_async_remote_copy(src_ref=st.at[me], dst_ref=st.at[me], send_sem=ss_sem.at[i],
                                            recv_sem=sr_sem.at[i], device_id={'tp': peer}, device_id_type=MESH)
        copy.start()
        stat_copies.append(copy)
    for copy in stat_copies:
        copy.wait_recv()
    top = jnp.maximum(jnp.maximum(st[0, 0], st[1, 0]), jnp.maximum(st[2, 0], st[3, 0]))
    norm = jnp.zeros((8, 128), F32)
    hit = jnp.zeros((8, 128), F32)
    for i in range(4):
        norm = norm + st[i, 1] * jnp.exp(st[i, 0] - top)
        hit = hit + st[i, 2]
    m = jnp.max(top, axis=0, keepdims=True)
    for shift in (32, 64):
        m = jnp.maximum(m, pltpu.roll(m, shift, 1))
    norm = jnp.sum(norm * jnp.exp(top - m), axis=0, keepdims=True)
    hit = jnp.sum(hit, axis=0, keepdims=True)
    for shift in (32, 64):
        norm = norm + pltpu.roll(norm, shift, 1)
        hit = hit + pltpu.roll(hit, shift, 1)
    log_norm = m + jnp.log(norm)
    stats_ref[...] = jnp.concatenate([log_norm, hit - log_norm, jnp.zeros((6, 128), F32)], axis=0)
    pick = lax.broadcasted_iota(jnp.int32, (tokens, 128), 0) == lax.broadcasted_iota(jnp.int32, (tokens, 128), 1)
    col = jnp.sum(jnp.where(pick, log_norm, 0.0), axis=1, keepdims=True)
    lncol_ref[...] = jnp.broadcast_to(col, (tokens, 128))

    for copy in stat_copies:
        copy.wait_send()

    @pl.loop(0, last)
    def _(k):
        x_copy(k, chunk(k)).wait_send()

    @pl.loop(0, nf)
    def _(k):
        a_copy(k, chunk(k)).wait_send()
        b_copy(k, chunk(k)).wait_send()

    for p in range(PIECES):
        x_piece(p).wait_send()
    a_copy(nf, tail_rows).wait_send()
    b_copy(nf, tail_rows).wait_send()
    x_copy(nf, tail_rows).wait_send()


def probs_kernel(block, vq, logits_ref, stats_ref, lncol_ref, ln_hbm, tl_hbm, probs_hbm, ln, tl, probs, sem, small_sem):
    tokens = ln.shape[1]
    ln[...] = stats_ref[0:1, :tokens]
    tl[...] = stats_ref[1:2, :tokens]
    copies = [pltpu.make_async_copy(ln, ln_hbm, small_sem.at[0]), pltpu.make_async_copy(tl, tl_hbm, small_sem.at[1])]
    log_norm = lncol_ref[:, 0:1]
    for i, start in enumerate(range(0, vq, block)):
        sl = pl.ds(start, min(block, vq - start))
        probs[:, sl] = jnp.exp(logits_ref[:, sl] - log_norm).astype(BF16)
        if i == 0:
            for copy in copies:
                copy.start()
        copies.append(pltpu.make_async_copy(probs.at[:, sl], probs_hbm.at[:, sl], sem.at[i]))
        copies[-1].start()
    for copy in copies:
        copy.wait()


def solution(mesh):
    def local_scores(hidden, final_gain, table, targets, temperature):
        tokens, hidden_size = hidden.shape
        vocab, width = table.shape
        vq = vocab // 4
        nf = vq // (G * R)
        rt = (vq - nf * G * R) // G
        packed = vq // G
        lanes = (vq + 127) // 128 * 128
        dims = (tokens, hidden_size, width, vq, nf, rt)
        vmem = pl.BlockSpec(memory_space=pltpu.VMEM)
        hbm = pl.BlockSpec(memory_space=pltpu.HBM)
        nsem = nf + PIECES
        logits, stats, lncol = pl.pallas_call(
            functools.partial(scores_kernel, dims),
            out_shape=(pltpu.VMEM((tokens, lanes), F32), pltpu.VMEM((8, 128), F32), pltpu.VMEM((tokens, 128), F32)),
            in_specs=[pl.BlockSpec(memory_space=pltpu.SMEM), hbm, hbm, hbm, hbm],
            out_specs=(vmem, vmem, vmem),
            scratch_shapes=[
                pltpu.VMEM((1, tokens), jnp.int32),
                pltpu.VMEM((tokens, hidden_size), BF16),
                pltpu.VMEM((hidden_size // 128, 128), BF16),
                pltpu.VMEM((hidden_size // 128, 128), F32),
                pltpu.VMEM((G * width, 128), BF16),
                pltpu.VMEM((NBUF, G * R, width), BF16),
                pltpu.VMEM((4, G * rt, width), BF16),
            ] + [pltpu.VMEM((packed, 128), F32)] * 7 + [
                pltpu.VMEM((4, 3, 8, 128), F32),
                pltpu.SemaphoreType.DMA((3,)),
                pltpu.SemaphoreType.DMA((NBUF,)),
                pltpu.SemaphoreType.DMA((4,)),
            ] + [pltpu.SemaphoreType.DMA((nsem,))] * 6 + [
                pltpu.SemaphoreType.DMA((3,)),
                pltpu.SemaphoreType.DMA((3,)),
            ],
            compiler_params=pltpu.CompilerParams(collective_id=0, has_side_effects=True,
                                                 vmem_limit_bytes=50 * 2 ** 20),
        )(temperature.reshape(1, 1), targets.reshape(1, tokens), hidden, final_gain.reshape(hidden_size // 128, 128), table)
        block = 4096
        log_norm, target_logprob, probs = pl.pallas_call(
            functools.partial(probs_kernel, block, vq),
            out_shape=(jax.ShapeDtypeStruct((1, tokens), F32),
                       jax.ShapeDtypeStruct((1, tokens), F32),
                       jax.ShapeDtypeStruct((tokens, vq), BF16)),
            in_specs=[vmem, vmem, vmem],
            out_specs=(hbm, hbm, hbm),
            scratch_shapes=[pltpu.VMEM((1, tokens), F32), pltpu.VMEM((1, tokens), F32),
                            pltpu.VMEM((tokens, vq), BF16),
                            pltpu.SemaphoreType.DMA((pl.cdiv(vq, block),)), pltpu.SemaphoreType.DMA((2,))],
            compiler_params=pltpu.CompilerParams(vmem_limit_bytes=8 * 2 ** 20),
        )(logits, stats, lncol)
        return log_norm.reshape(tokens), target_logprob.reshape(tokens), probs

    return jax.shard_map(local_scores, mesh=mesh,
                         in_specs=(P('dp', None), P(None), P(None, 'tp'), P('dp'), P()),
                         out_specs=(P('dp'), P('dp'), P('dp', 'tp')),
                         check_vma=False)
```

time: 114 us -> 105 us (0.921)
  Pallas kernels: 110 us -> 104 us
  local copies, waits for them, and re-layouts: 2.55 us -> 0 us
    pallas_call x2, Pallas kernels: 110 us -> 104 us  [the longest x1 102 us: local_scores(): pl.pallas_call(functools.partial(scores_kernel, dims), out_shape=(pltpu.V...]
    reshape x1 -> x0, local copies, waits for them, and re-layouts: 1.3 us -> none  [local_scores(): final_gain.reshape(1, hidden_size)]
    another operation x2 -> x0, local copies, waits for them, and re-layouts: 1.25 us -> none  [local_scores(): tgt = jnp.tile(targets, G).reshape(1, G * tokens)]
where the time goes in v2:
time: 105 us
  Pallas kernels  104 us (99%)
  between operations  1.29 us (1%)
    pallas_call x1, Pallas kernels, local_scores(): pl.pallas_call(functools.partial(scores_kernel, dims), out_shape=(pltpu.V...  102 us

profile of v2, /device:TPU:0, one launch (start us, length us, event | category | flops | bytes accessed | tf_op | source)
XLA Modules:
  0.0 105.1 jit_solution(17533718462304107887)
XLA Ops:
  1.3 102.2 %shard_map.76 = (f32[32,32128]{1,0:T(8,128)S(1)}, f32[8,128]{1,0:T(8,128)S(1)}, f32[32,128]{1,0:T(8,128)S(1)}) custom-call(f32[1,1]{1,0:T(1,128)} %bitcast.5.temp_ref, s32[1,32]{1,0:T(1,128)} %bitcast.7, bf16[32,3072]{1,0:T(8,128)(2,1)} %hid_hbm.1, bf16[24,128]{1,0:T(8,128)(2,1)} %bitcast.6, bf16[128256,768]{1,0:T(8,128)(2,1)} %table.1), custom_call_target="tpu_custom_call" | custom-call | tf_op jit(solution)/shard_map/pallas_call | solution.py:307
  103.5 1.5 %shard_map.77 = (f32[1,32]{1,0:T(1,128)}, f32[1,32]{1,0:T(1,128)}, bf16[32,32064]{1,0:T(8,128)(2,1)}) custom-call(f32[32,32128]{1,0:T(8,128)S(1)} %get-tuple-element.9.logits_ref, f32[8,128]{1,0:T(8,128)S(1)} %get-tuple-element.10.stats_ref, f32[32,128]{1,0:T(8,128)S(1)} %get-tuple-element.11.lncol_ref), custom_call_target="tpu_custom_call" | custom-call | tf_op jit(solution)/shard_map/pallas_call | solution.py:333

commit v3 on v2

v3 whole, which is shorter than its diff:
```python
import functools

import jax
import jax.numpy as jnp
from jax import lax
from jax.experimental import pallas as pl
from jax.experimental.pallas import tpu as pltpu
from jax.sharding import PartitionSpec as P

NORM_EPS = 1e-6
MESH = pl.DeviceIdType.MESH
F32 = jnp.float32
BF16 = jnp.bfloat16
G = 4
R = 256
NR = 3
NL = 2
LAG = 2
LATE = 4
PIECES = 2


def scores_kernel(dims, temp_ref, tgt_hbm, hid_hbm, gain_hbm, table, logits_ref, stats_ref, lncol_ref,
                  tgt_ref, hid, gain, gain32, w, ring_r, ring_l, tail, ps, po, ls, lo, ra, rb, rx, acc, st,
                  in_sem, r_sem, l_sem, tail_sem, as_sem, ar_sem, bs_sem, br_sem, xs_sem, xr_sem, ss_sem, sr_sem):
    tokens, hidden_size, width, vq, nf, rt = dims
    me = lax.axis_index('tp')
    x = me // 2
    c = me % 2
    sib = 2 * x + (1 - c)
    xpeer = 2 * (1 - x) + c
    diag = 2 * (1 - x) + (1 - c)
    rows = G * R
    trows = G * rt
    last = nf - 1

    def quarter(chip, half):
        return (2 * chip + ((1 - c) if half == 0 else c)) * vq

    def r_copy(k, half):
        start = pl.multiple_of(quarter(1 - x, half) + k * rows, 64)
        return pltpu.make_async_copy(table.at[pl.ds(start, rows)], ring_r.at[k % NR, half], r_sem.at[k % NR, half])

    def l_copy(k, half):
        start = pl.multiple_of(quarter(x, half) + k * rows, 64)
        return pltpu.make_async_copy(table.at[pl.ds(start, rows)], ring_l.at[k % NL, half], l_sem.at[k % NL, half])

    def tail_copy(i):
        start = pl.multiple_of(quarter((1 - x) if i < 2 else x, i % 2) + nf * rows, 64)
        return pltpu.make_async_copy(table.at[pl.ds(start, trows)], tail.at[i], tail_sem.at[i])

    def chunk(k):
        return pl.ds(pl.multiple_of(k * R, R), R)

    tail_rows = pl.ds(nf * R, rt)

    def remote(src, dst, send, recv, k, sl, dev):
        return pltpu.make_async_remote_copy(src_ref=src.at[sl], dst_ref=dst.at[sl], send_sem=send.at[k],
                                            recv_sem=recv.at[k], device_id={'tp': dev}, device_id_type=MESH)

    def a_copy(k, sl):
        return remote(ps, ra, as_sem, ar_sem, k, sl, sib)

    def b_copy(k, sl):
        return remote(ls, rb, bs_sem, br_sem, k, sl, sib)

    def x_copy(k, sl):
        return remote(po, rx, xs_sem, xr_sem, k, sl, xpeer)

    piece = R // PIECES

    def x_piece(p):
        return x_copy(last if p == 0 else nf + p, pl.ds(last * R + p * piece, piece))

    hid_copy = pltpu.make_async_copy(hid_hbm, hid, in_sem.at[0])
    gain_copy = pltpu.make_async_copy(gain_hbm, gain, in_sem.at[1])
    tgt_copy = pltpu.make_async_copy(tgt_hbm, tgt_ref, in_sem.at[2])
    hid_copy.start()
    gain_copy.start()
    tgt_copy.start()
    tail_copy(0).start()
    tail_copy(1).start()

    barrier = pltpu.get_barrier_semaphore()
    for peer in (sib, xpeer, diag):
        pl.semaphore_signal(barrier, inc=1, device_id={'tp': peer}, device_id_type=MESH)

    hid_copy.wait()
    gain_copy.wait()
    for k in range(NR):
        r_copy(k, 0).start()
        r_copy(k, 1).start()
    tail_copy(2).start()
    tail_copy(3).start()

    hf = hid[...].astype(F32)
    inv = lax.rsqrt(jnp.mean(hf * hf, axis=-1, keepdims=True) + NORM_EPS)
    cols = pl.ds(pl.multiple_of(me * width, 128), width)
    gain32[...] = gain[...].astype(F32)
    scaled = hid[:, cols].astype(F32) * inv
    u = jnp.concatenate([scaled[:, j * 128:(j + 1) * 128] * gain32[pl.ds(me * (width // 128) + j, 1), :]
                         for j in range(width // 128)], axis=1).astype(BF16).astype(F32)
    u_t = jnp.concatenate([u] * G, axis=0).T
    group = lax.broadcasted_iota(jnp.int32, (width, 128), 1) // tokens
    for g in range(G):
        w[g * width:(g + 1) * width, :] = jnp.where(group == g, u_t, 0.0).astype(BF16)
    acc[0] = jnp.full((8, 128), -jnp.inf, F32)
    acc[1] = jnp.zeros((8, 128), F32)
    acc[2] = jnp.zeros((8, 128), F32)
    temp = temp_ref[0, 0]
    lane_group = lax.broadcasted_iota(jnp.int32, (1, 128), 1) // tokens
    tgt_copy.wait()
    tgt = jnp.concatenate([tgt_ref[...]] * G, axis=1) - me * vq

    def packed_dot(views, n):
        total = None
        for g in range(G):
            parts = [view[g * n:(g + 1) * n, :] for view in views]
            lhs = parts[0] if len(parts) == 1 else jnp.concatenate(parts, axis=0)
            part = jnp.dot(lhs, w[g * width:(g + 1) * width, :], preferred_element_type=F32)
            total = part if total is None else total + part
        return total

    def r_dot(k, half, dst):
        r_copy(k, half).wait()
        dst[chunk(k), :] = packed_dot([ring_r.at[k % NR, half]], R)

        @pl.when(k + NR < nf)
        def _():
            r_copy(k + NR, half).start()

    def l_dot(k):
        l_copy(k, 0).wait()
        l_copy(k, 1).wait()
        both = packed_dot([ring_l.at[k % NL, 0], ring_l.at[k % NL, 1]], R)
        ls[chunk(k), :] = both[:R]
        lo[chunk(k), :] = both[R:]

        @pl.when(k + NL < nf)
        def _():
            l_copy(k + NL, 0).start()
            l_copy(k + NL, 1).start()

    def add_sibling(k, sl):
        a_copy(k, sl).wait_recv()
        po[sl, :] = po[sl, :] + ra[sl, :]

    def update(sl, n, base, stride):
        t = (lo[sl, :] + rb[sl, :] + rx[sl, :]) / temp
        t3 = t.reshape(n // 8, 8, 128)
        m_old = acc[0]
        m_new = jnp.maximum(m_old, jnp.max(t3, axis=0))
        acc[0] = m_new
        acc[1] = acc[1] * jnp.exp(m_old - m_new) + jnp.sum(jnp.exp(t3 - m_new), axis=0)
        row = lax.broadcasted_iota(jnp.int32, (n, 128), 0)
        hit = row == (tgt - base - lane_group * stride)
        acc[2] += jnp.sum(jnp.where(hit, t, 0.0).reshape(n // 8, 8, 128), axis=0)
        return t

    def put(t, n, base, stride):
        tt = t.T
        for g in range(G):
            logits_ref[:, pl.ds(pl.multiple_of(base + g * stride, 128), n)] = tt[g * tokens:(g + 1) * tokens, :]

    def finish_tail():
        b_copy(nf, tail_rows).wait_recv()
        x_copy(nf, tail_rows).wait_recv()
        t = update(tail_rows, rt, nf * rows, rt)
        tt = jnp.concatenate([t, jnp.zeros((128 - rt, 128), F32)], axis=0).T
        parts = [tt[g * tokens:(g + 1) * tokens, :] for g in range(G)]
        lane = lax.broadcasted_iota(jnp.int32, (tokens, 128), 1)
        for i in range((G * rt + 127) // 128):
            tile = jnp.zeros((tokens, 128), F32)
            for g in range(G):
                off = g * rt - i * 128
                if off <= -rt or off >= 128:
                    continue
                moved = pltpu.roll(parts[g], off % 128, 1) if off % 128 else parts[g]
                tile = jnp.where((lane >= off) & (lane < off + rt), moved, tile)
            logits_ref[:, nf * rows + i * 128:nf * rows + (i + 1) * 128] = tile
        a_copy(nf, tail_rows).wait_send()
        b_copy(nf, tail_rows).wait_send()
        x_copy(nf, tail_rows).wait_send()

    tail_copy(0).wait()
    ps[tail_rows, :] = packed_dot([tail.at[0]], rt)
    tail_copy(1).wait()
    po[tail_rows, :] = packed_dot([tail.at[1]], rt)
    pl.semaphore_wait(barrier, 3)
    a_copy(nf, tail_rows).start()

    @pl.loop(0, nf + LATE - 1)
    def _(j):
        @pl.when(j < nf)
        def _():
            r_dot(j, 0, ps)
            a_copy(j, chunk(j)).start()

        @pl.when(j == 0)
        def _():
            add_sibling(nf, tail_rows)
            x_copy(nf, tail_rows).start()

        @pl.when(jnp.logical_and(j > 0, j <= nf))
        def _():
            add_sibling(j - 1, chunk(j - 1))

        @pl.when(j == 1)
        def _():
            x_copy(j - 1, chunk(j - 1)).start()

        @pl.when(j < nf)
        def _():
            r_dot(j, 1, po)

        @pl.when(jnp.logical_and(j > 1, j < nf))
        def _():
            x_copy(j - 1, chunk(j - 1)).start()

        @pl.when(j < NL)
        def _():
            l_copy(j, 0).start()
            l_copy(j, 1).start()

        @pl.when(jnp.logical_and(j > LAG, j <= nf + LAG))
        def _():
            b_copy(j - LAG - 1, chunk(j - LAG - 1)).start()

        @pl.when(jnp.logical_and(j >= LAG, j < nf + LAG))
        def _():
            l_dot(j - LAG)

        @pl.when(j == nf)
        def _():
            for p in range(PIECES):
                x_piece(p).start()

        @pl.when(j == 4)
        def _():
            tail_copy(2).wait()
            tail_copy(3).wait()
            both = packed_dot([tail.at[2], tail.at[3]], rt)
            ls[tail_rows, :] = both[:rt]
            lo[tail_rows, :] = both[rt:]

        @pl.when(j == 5)
        def _():
            b_copy(nf, tail_rows).start()

        @pl.when(j == 8)
        def _():
            finish_tail()

        @pl.when(j >= LATE)
        def _():
            k = j - LATE
            b_copy(k, chunk(k)).wait_recv()
            x_copy(k, chunk(k)).wait_recv()
            put(update(chunk(k), R, k * rows, R), R, k * rows, R)
            a_copy(k, chunk(k)).wait_send()
            b_copy(k, chunk(k)).wait_send()

            @pl.when(k > 0)
            def _():
                x_copy(k - 1, chunk(k - 1)).wait_send()

    x_copy(last - 1, chunk(last - 1)).wait_send()
    a_copy(last, chunk(last)).wait_send()
    b_copy(last, chunk(last)).wait_send()
    b_copy(last, chunk(last)).wait_recv()
    for p in range(PIECES):
        x_piece(p).wait_recv()
        t = update(pl.ds(last * R + p * piece, piece), piece, last * rows + p * piece, R)
        put(t, piece, last * rows + p * piece, R)

    m = jnp.max(acc[0], axis=0, keepdims=True)
    norm = jnp.sum(acc[1] * jnp.exp(acc[0] - m), axis=0, keepdims=True)
    hit = jnp.sum(acc[2], axis=0, keepdims=True)
    st[me] = jnp.concatenate([m, norm, hit, jnp.zeros((5, 128), F32)], axis=0)
    for p in range(PIECES):
        x_piece(p).wait_send()
    stat_copies = []
    for i, peer in enumerate((xpeer, diag, sib)):
        copy = pltpu.make_async_remote_copy(src_ref=st.at[me], dst_ref=st.at[me], send_sem=ss_sem.at[i],
                                            recv_sem=sr_sem.at[i], device_id={'tp': peer}, device_id_type=MESH)
        copy.start()
        stat_copies.append(copy)
    for copy in stat_copies:
        copy.wait_send()
    for copy in stat_copies:
        copy.wait_recv()
    ms, ns, hit = [], [], jnp.zeros((1, 128), F32)
    for i in range(4):
        hit = hit + st[i, 2:3, :]
        for shift in range(0, G * tokens, tokens):
            ms.append(pltpu.roll(st[i, 0:1, :], shift, 1) if shift else st[i, 0:1, :])
            ns.append(pltpu.roll(st[i, 1:2, :], shift, 1) if shift else st[i, 1:2, :])
    hit = sum(pltpu.roll(hit, shift, 1) for shift in range(tokens, G * tokens, tokens)) + hit
    top = functools.reduce(jnp.maximum, ms)
    norm = sum(n * jnp.exp(m - top) for n, m in zip(ns, ms))
    log_norm = top + jnp.log(norm)
    stats_ref[...] = jnp.concatenate([log_norm, hit - log_norm, jnp.zeros((6, 128), F32)], axis=0)
    pick = lax.broadcasted_iota(jnp.int32, (tokens, 128), 0) == lax.broadcasted_iota(jnp.int32, (tokens, 128), 1)
    col = jnp.sum(jnp.where(pick, log_norm, 0.0), axis=1, keepdims=True)
    lncol_ref[...] = jnp.broadcast_to(col, (tokens, 128))


def probs_kernel(block, vq, logits_ref, stats_ref, lncol_ref, ln_hbm, tl_hbm, probs_hbm, ln, tl, probs, sem, small_sem):
    tokens = ln.shape[1]
    ln[...] = stats_ref[0:1, :tokens]
    tl[...] = stats_ref[1:2, :tokens]
    copies = [pltpu.make_async_copy(ln, ln_hbm, small_sem.at[0]), pltpu.make_async_copy(tl, tl_hbm, small_sem.at[1])]
    log_norm = lncol_ref[:, 0:1]
    for i, start in enumerate(range(0, vq, block)):
        sl = pl.ds(start, min(block, vq - start))
        probs[:, sl] = jnp.exp(logits_ref[:, sl] - log_norm).astype(BF16)
        if i == 0:
            for copy in copies:
                copy.start()
        copies.append(pltpu.make_async_copy(probs.at[:, sl], probs_hbm.at[:, sl], sem.at[i]))
        copies[-1].start()
    for copy in copies:
        copy.wait()


def solution(mesh):
    def local_scores(hidden, final_gain, table, targets, temperature):
        tokens, hidden_size = hidden.shape
        vocab, width = table.shape
        vq = vocab // 4
        nf = vq // (G * R)
        rt = (vq - nf * G * R) // G
        packed = vq // G
        lanes = (vq + 127) // 128 * 128
        dims = (tokens, hidden_size, width, vq, nf, rt)
        vmem = pl.BlockSpec(memory_space=pltpu.VMEM)
        hbm = pl.BlockSpec(memory_space=pltpu.HBM)
        nsem = nf + PIECES
        logits, stats, lncol = pl.pallas_call(
            functools.partial(scores_kernel, dims),
            out_shape=(pltpu.VMEM((tokens, lanes), F32), pltpu.VMEM((8, 128), F32), pltpu.VMEM((tokens, 128), F32)),
            in_specs=[pl.BlockSpec(memory_space=pltpu.SMEM), hbm, hbm, hbm, hbm],
            out_specs=(vmem, vmem, vmem),
            scratch_shapes=[
                pltpu.VMEM((1, tokens), jnp.int32),
                pltpu.VMEM((tokens, hidden_size), BF16),
                pltpu.VMEM((hidden_size // 128, 128), BF16),
                pltpu.VMEM((hidden_size // 128, 128), F32),
                pltpu.VMEM((G * width, 128), BF16),
                pltpu.VMEM((NR, 2, G * R, width), BF16),
                pltpu.VMEM((NL, 2, G * R, width), BF16),
                pltpu.VMEM((4, G * rt, width), BF16),
            ] + [pltpu.VMEM((packed, 128), F32)] * 7 + [
                pltpu.VMEM((3, 8, 128), F32),
                pltpu.VMEM((4, 8, 128), F32),
                pltpu.SemaphoreType.DMA((3,)),
                pltpu.SemaphoreType.DMA((NR, 2)),
                pltpu.SemaphoreType.DMA((NL, 2)),
                pltpu.SemaphoreType.DMA((4,)),
            ] + [pltpu.SemaphoreType.DMA((nsem,))] * 6 + [
                pltpu.SemaphoreType.DMA((3,)),
                pltpu.SemaphoreType.DMA((3,)),
            ],
            compiler_params=pltpu.CompilerParams(collective_id=0, has_side_effects=True,
                                                 vmem_limit_bytes=54 * 2 ** 20),
        )(temperature.reshape(1, 1), targets.reshape(1, tokens), hidden, final_gain.reshape(hidden_size // 128, 128), table)
        block = 4096
        log_norm, target_logprob, probs = pl.pallas_call(
            functools.partial(probs_kernel, block, vq),
            out_shape=(jax.ShapeDtypeStruct((1, tokens), F32),
                       jax.ShapeDtypeStruct((1, tokens), F32),
                       jax.ShapeDtypeStruct((tokens, vq), BF16)),
            in_specs=[vmem, vmem, vmem],
            out_specs=(hbm, hbm, hbm),
            scratch_shapes=[pltpu.VMEM((1, tokens), F32), pltpu.VMEM((1, tokens), F32),
                            pltpu.VMEM((tokens, vq), BF16),
                            pltpu.SemaphoreType.DMA((pl.cdiv(vq, block),)), pltpu.SemaphoreType.DMA((2,))],
            compiler_params=pltpu.CompilerParams(vmem_limit_bytes=8 * 2 ** 20),
        )(logits, stats, lncol)
        return log_norm.reshape(tokens), target_logprob.reshape(tokens), probs

    return jax.shard_map(local_scores, mesh=mesh,
                         in_specs=(P('dp', None), P(None), P(None, 'tp'), P('dp'), P()),
                         out_specs=(P('dp'), P('dp'), P('dp', 'tp')),
                         check_vma=False)
```

time: 105 us -> 102 us (0.971)
  Pallas kernels: 104 us -> 101 us
    pallas_call x1, Pallas kernels: 102 us -> 99.5 us  [local_scores(): pl.pallas_call(functools.partial(scores_kernel, dims), out_shape=(pltpu.V...]
where the time goes in v3:
time: 102 us
  Pallas kernels  101 us (99%)
  between operations  1.29 us (1%)
    pallas_call x1, Pallas kernels, local_scores(): pl.pallas_call(functools.partial(scores_kernel, dims), out_shape=(pltpu.V...  99.5 us

profile of v3, /device:TPU:0, one launch (start us, length us, event | category | flops | bytes accessed | tf_op | source)
XLA Modules:
  0.0 102.3 jit_solution(1644200502319410860)
XLA Ops:
  1.3 99.5 %shard_map.76 = (f32[32,32128]{1,0:T(8,128)S(1)}, f32[8,128]{1,0:T(8,128)S(1)}, f32[32,128]{1,0:T(8,128)S(1)}) custom-call(f32[1,1]{1,0:T(1,128)} %bitcast.5.temp_ref, s32[1,32]{1,0:T(1,128)} %bitcast.7, bf16[32,3072]{1,0:T(8,128)(2,1)} %hid_hbm.1, bf16[24,128]{1,0:T(8,128)(2,1)} %bitcast.6, bf16[128256,768]{1,0:T(8,128)(2,1)} %table.1), custom_call_target="tpu_custom_call" | custom-call | tf_op jit(solution)/shard_map/pallas_call | solution.py:339
  100.8 1.5 %shard_map.77 = (f32[1,32]{1,0:T(1,128)}, f32[1,32]{1,0:T(1,128)}, bf16[32,32064]{1,0:T(8,128)(2,1)}) custom-call(f32[32,32128]{1,0:T(8,128)S(1)} %get-tuple-element.9.logits_ref, f32[8,128]{1,0:T(8,128)S(1)} %get-tuple-element.10.stats_ref, f32[32,128]{1,0:T(8,128)S(1)} %get-tuple-element.11.lncol_ref), custom_call_target="tpu_custom_call" | custom-call | tf_op jit(solution)/shard_map/pallas_call | solution.py:368

commit v4 on v3

--- a/solution.py
+++ b/solution.py
@@ -17,12 +17,12 @@
 NL = 2
 LAG = 2
 LATE = 4
-PIECES = 2
-
-
-def scores_kernel(dims, temp_ref, tgt_hbm, hid_hbm, gain_hbm, table, logits_ref, stats_ref, lncol_ref,
-                  tgt_ref, hid, gain, gain32, w, ring_r, ring_l, tail, ps, po, ls, lo, ra, rb, rx, acc, st,
-                  in_sem, r_sem, l_sem, tail_sem, as_sem, ar_sem, bs_sem, br_sem, xs_sem, xr_sem, ss_sem, sr_sem):
+NA, NB, NS, NX = 5, 5, 5, 2 * LATE
+
+
+def scores_kernel(dims, temp_ref, tgt_hbm, hid_hbm, gain_hbm, table, logits_ref, stats_ref, scale_ref,
+                  tgt_ref, hid, gain, gain32, w, ring_r, ring_l, tail, ps, po, ls, lo, ra, rb, rx, rx2, acc, st,
+                  in_sem, r_sem, l_sem, tail_sem, as_sem, ar_sem, bs_sem, br_sem, xs_sem, xr_sem, one_sem, ss_sem, sr_sem):
     tokens, hidden_size, width, vq, nf, rt = dims
     me = lax.axis_index('tp')
     x = me // 2
@@ -54,23 +54,37 @@
 
     tail_rows = pl.ds(nf * R, rt)
 
-    def remote(src, dst, send, recv, k, sl, dev):
-        return pltpu.make_async_remote_copy(src_ref=src.at[sl], dst_ref=dst.at[sl], send_sem=send.at[k],
-                                            recv_sem=recv.at[k], device_id={'tp': dev}, device_id_type=MESH)
-
-    def a_copy(k, sl):
-        return remote(ps, ra, as_sem, ar_sem, k, sl, sib)
-
-    def b_copy(k, sl):
-        return remote(ls, rb, bs_sem, br_sem, k, sl, sib)
-
-    def x_copy(k, sl):
-        return remote(po, rx, xs_sem, xr_sem, k, sl, xpeer)
-
-    piece = R // PIECES
+    def remote(src, dst, send, recv, dev):
+        return pltpu.make_async_remote_copy(src_ref=src, dst_ref=dst, send_sem=send, recv_sem=recv,
+                                            device_id={'tp': dev}, device_id_type=MESH)
+
+    def a_copy(k):
+        sl = chunk(k)
+        return remote(ps.at[sl], ra.at[sl], as_sem.at[k % 2], ar_sem.at[k % NA], sib)
+
+    def b_copy(k):
+        sl = chunk(k)
+        return remote(ls.at[sl], rb.at[sl], bs_sem.at[k % 2], br_sem.at[k % NB], sib)
+
+    def x_copy(k):
+        sl = chunk(k)
+        return remote(po.at[sl], rx.at[sl], xs_sem.at[k % NS], xr_sem.at[k % NX], xpeer)
+
+    def b_tail():
+        return remote(ls.at[tail_rows], rb.at[tail_rows], one_sem.at[0], one_sem.at[1], sib)
+
+    def x_tail():
+        return remote(po.at[tail_rows], rx.at[tail_rows], one_sem.at[2], one_sem.at[3], xpeer)
+
+    def x2_tail():
+        return remote(ps.at[tail_rows], rx2, one_sem.at[4], one_sem.at[5], diag)
+
+    piece = R // 2
 
     def x_piece(p):
-        return x_copy(last if p == 0 else nf + p, pl.ds(last * R + p * piece, piece))
+        sl = pl.ds(last * R + p * piece, piece)
+        send, recv = (one_sem.at[6], one_sem.at[7]) if p else (xs_sem.at[last % NS], xr_sem.at[last % NX])
+        return remote(po.at[sl], rx.at[sl], send, recv, xpeer)
 
     hid_copy = pltpu.make_async_copy(hid_hbm, hid, in_sem.at[0])
     gain_copy = pltpu.make_async_copy(gain_hbm, gain, in_sem.at[1])
@@ -141,12 +155,14 @@
             l_copy(k + NL, 0).start()
             l_copy(k + NL, 1).start()
 
-    def add_sibling(k, sl):
-        a_copy(k, sl).wait_recv()
+    def add_sibling(k):
+        sl = chunk(k)
+        a_copy(k).wait_recv()
         po[sl, :] = po[sl, :] + ra[sl, :]
 
-    def update(sl, n, base, stride):
-        t = (lo[sl, :] + rb[sl, :] + rx[sl, :]) / temp
+    def update(sl, n, base, stride, crossed=None):
+        z = lo[sl, :] + rb[sl, :] + rx[sl, :]
+        t = (z if crossed is None else z + crossed) / temp
         t3 = t.reshape(n // 8, 8, 128)
         m_old = acc[0]
         m_new = jnp.maximum(m_old, jnp.max(t3, axis=0))
@@ -163,9 +179,10 @@
             logits_ref[:, pl.ds(pl.multiple_of(base + g * stride, 128), n)] = tt[g * tokens:(g + 1) * tokens, :]
 
     def finish_tail():
-        b_copy(nf, tail_rows).wait_recv()
-        x_copy(nf, tail_rows).wait_recv()
-        t = update(tail_rows, rt, nf * rows, rt)
+        b_tail().wait_recv()
+        x_tail().wait_recv()
+        x2_tail().wait_recv()
+        t = update(tail_rows, rt, nf * rows, rt, rx2[...])
         tt = jnp.concatenate([t, jnp.zeros((128 - rt, 128), F32)], axis=0).T
         parts = [tt[g * tokens:(g + 1) * tokens, :] for g in range(G)]
         lane = lax.broadcasted_iota(jnp.int32, (tokens, 128), 1)
@@ -178,36 +195,37 @@
                 moved = pltpu.roll(parts[g], off % 128, 1) if off % 128 else parts[g]
                 tile = jnp.where((lane >= off) & (lane < off + rt), moved, tile)
             logits_ref[:, nf * rows + i * 128:nf * rows + (i + 1) * 128] = tile
-        a_copy(nf, tail_rows).wait_send()
-        b_copy(nf, tail_rows).wait_send()
-        x_copy(nf, tail_rows).wait_send()
+        b_tail().wait_send()
+        x_tail().wait_send()
+        x2_tail().wait_send()
 
     tail_copy(0).wait()
     ps[tail_rows, :] = packed_dot([tail.at[0]], rt)
     tail_copy(1).wait()
     po[tail_rows, :] = packed_dot([tail.at[1]], rt)
     pl.semaphore_wait(barrier, 3)
-    a_copy(nf, tail_rows).start()
+    x_tail().start()
+    x2_tail().start()
 
     @pl.loop(0, nf + LATE - 1)
     def _(j):
         @pl.when(j < nf)
         def _():
             r_dot(j, 0, ps)
-            a_copy(j, chunk(j)).start()
-
-        @pl.when(j == 0)
-        def _():
-            add_sibling(nf, tail_rows)
-            x_copy(nf, tail_rows).start()
+
+            @pl.when(j >= 2)
+            def _():
+                a_copy(j - 2).wait_send()
+
+            a_copy(j).start()
 
         @pl.when(jnp.logical_and(j > 0, j <= nf))
         def _():
-            add_sibling(j - 1, chunk(j - 1))
+            add_sibling(j - 1)
 
         @pl.when(j == 1)
         def _():
-            x_copy(j - 1, chunk(j - 1)).start()
+            x_copy(j - 1).start()
 
         @pl.when(j < nf)
         def _():
@@ -215,7 +233,7 @@
 
         @pl.when(jnp.logical_and(j > 1, j < nf))
         def _():
-            x_copy(j - 1, chunk(j - 1)).start()
+            x_copy(j - 1).start()
 
         @pl.when(j < NL)
         def _():
@@ -224,7 +242,13 @@
 
         @pl.when(jnp.logical_and(j > LAG, j <= nf + LAG))
         def _():
-            b_copy(j - LAG - 1, chunk(j - LAG - 1)).start()
+            k = j - LAG - 1
+
+            @pl.when(k >= 2)
+            def _():
+                b_copy(k - 2).wait_send()
+
+            b_copy(k).start()
 
         @pl.when(jnp.logical_and(j >= LAG, j < nf + LAG))
         def _():
@@ -232,7 +256,7 @@
 
         @pl.when(j == nf)
         def _():
-            for p in range(PIECES):
+            for p in range(2):
                 x_piece(p).start()
 
         @pl.when(j == 4)
@@ -245,7 +269,7 @@
 
         @pl.when(j == 5)
         def _():
-            b_copy(nf, tail_rows).start()
+            b_tail().start()
 
         @pl.when(j == 8)
         def _():
@@ -254,21 +278,20 @@
         @pl.when(j >= LATE)
         def _():
             k = j - LATE
-            b_copy(k, chunk(k)).wait_recv()
-            x_copy(k, chunk(k)).wait_recv()
+            b_copy(k).wait_recv()
+            x_copy(k).wait_recv()
             put(update(chunk(k), R, k * rows, R), R, k * rows, R)
-            a_copy(k, chunk(k)).wait_send()
-            b_copy(k, chunk(k)).wait_send()
 
             @pl.when(k > 0)
             def _():
-                x_copy(k - 1, chunk(k - 1)).wait_send()
-
-    x_copy(last - 1, chunk(last - 1)).wait_send()
-    a_copy(last, chunk(last)).wait_send()
-    b_copy(last, chunk(last)).wait_send()
-    b_copy(last, chunk(last)).wait_recv()
-    for p in range(PIECES):
+                x_copy(k - 1).wait_send()
+
+    for k in (last - 1, last):
+        a_copy(k).wait_send()
+        b_copy(k).wait_send()
+    x_copy(last - 1).wait_send()
+    b_copy(last).wait_recv()
+    for p in range(2):
         x_piece(p).wait_recv()
         t = update(pl.ds(last * R + p * piece, piece), piece, last * rows + p * piece, R)
         put(t, piece, last * rows + p * piece, R)
@@ -277,7 +300,7 @@
     norm = jnp.sum(acc[1] * jnp.exp(acc[0] - m), axis=0, keepdims=True)
     hit = jnp.sum(acc[2], axis=0, keepdims=True)
     st[me] = jnp.concatenate([m, norm, hit, jnp.zeros((5, 128), F32)], axis=0)
-    for p in range(PIECES):
+    for p in range(2):
         x_piece(p).wait_send()
     stat_copies = []
     for i, peer in enumerate((xpeer, diag, sib)):
@@ -285,6 +308,21 @@
                                             recv_sem=sr_sem.at[i], device_id={'tp': peer}, device_id_type=MESH)
         copy.start()
         stat_copies.append(copy)
+    pick = lax.broadcasted_iota(jnp.int32, (tokens, 128), 0) == lax.broadcasted_iota(jnp.int32, (tokens, 128), 1)
+
+    def column(row):
+        return jnp.sum(jnp.where(pick, row, 0.0), axis=1, keepdims=True)
+
+    own = functools.reduce(jnp.maximum, [pltpu.roll(m, shift, 1) for shift in range(tokens, G * tokens, tokens)], m)
+    own_col = column(own)
+
+    @pl.loop(0, nf)
+    def _(k):
+        sl = pl.ds(pl.multiple_of(k * rows, 128), rows)
+        logits_ref[:, sl] = jnp.exp(logits_ref[:, sl] - own_col)
+
+    sl = pl.ds(nf * rows, logits_ref.shape[1] - nf * rows)
+    logits_ref[:, sl] = jnp.exp(logits_ref[:, sl] - own_col)
     for copy in stat_copies:
         copy.wait_send()
     for copy in stat_copies:
@@ -300,25 +338,23 @@
     norm = sum(n * jnp.exp(m - top) for n, m in zip(ns, ms))
     log_norm = top + jnp.log(norm)
     stats_ref[...] = jnp.concatenate([log_norm, hit - log_norm, jnp.zeros((6, 128), F32)], axis=0)
-    pick = lax.broadcasted_iota(jnp.int32, (tokens, 128), 0) == lax.broadcasted_iota(jnp.int32, (tokens, 128), 1)
-    col = jnp.sum(jnp.where(pick, log_norm, 0.0), axis=1, keepdims=True)
-    lncol_ref[...] = jnp.broadcast_to(col, (tokens, 128))
-
-
-def probs_kernel(block, vq, logits_ref, stats_ref, lncol_ref, ln_hbm, tl_hbm, probs_hbm, ln, tl, probs, sem, small_sem):
+    scale_ref[...] = jnp.broadcast_to(column(jnp.exp(own - log_norm)), (tokens, 128))
+
+
+def probs_kernel(block, vq, exp_ref, stats_ref, scale_ref, ln_hbm, tl_hbm, probs_hbm, ln, tl, probs, sem, small_sem):
     tokens = ln.shape[1]
     ln[...] = stats_ref[0:1, :tokens]
     tl[...] = stats_ref[1:2, :tokens]
     copies = [pltpu.make_async_copy(ln, ln_hbm, small_sem.at[0]), pltpu.make_async_copy(tl, tl_hbm, small_sem.at[1])]
-    log_norm = lncol_ref[:, 0:1]
+    scale = scale_ref[:, 0:1]
     for i, start in enumerate(range(0, vq, block)):
         sl = pl.ds(start, min(block, vq - start))
-        probs[:, sl] = jnp.exp(logits_ref[:, sl] - log_norm).astype(BF16)
+        probs[:, sl] = (exp_ref[:, sl] * scale).astype(BF16)
         if i == 0:
             for copy in copies:
                 copy.start()
-        copies.append(pltpu.make_async_copy(probs.at[:, sl], probs_hbm.at[:, sl], sem.at[i]))
-        copies[-1].start()
+        pltpu.make_async_copy(probs.at[:, sl], probs_hbm.at[:, sl], sem.at[0]).start()
+    copies.append(pltpu.make_async_copy(probs, probs_hbm, sem.at[0]))
     for copy in copies:
         copy.wait()
 
@@ -335,8 +371,7 @@
         dims = (tokens, hidden_size, width, vq, nf, rt)
         vmem = pl.BlockSpec(memory_space=pltpu.VMEM)
         hbm = pl.BlockSpec(memory_space=pltpu.HBM)
-        nsem = nf + PIECES
-        logits, stats, lncol = pl.pallas_call(
+        exps, stats, scale = pl.pallas_call(
             functools.partial(scores_kernel, dims),
             out_shape=(pltpu.VMEM((tokens, lanes), F32), pltpu.VMEM((8, 128), F32), pltpu.VMEM((tokens, 128), F32)),
             in_specs=[pl.BlockSpec(memory_space=pltpu.SMEM), hbm, hbm, hbm, hbm],
@@ -351,13 +386,14 @@
                 pltpu.VMEM((NL, 2, G * R, width), BF16),
                 pltpu.VMEM((4, G * rt, width), BF16),
             ] + [pltpu.VMEM((packed, 128), F32)] * 7 + [
+                pltpu.VMEM((rt, 128), F32),
                 pltpu.VMEM((3, 8, 128), F32),
                 pltpu.VMEM((4, 8, 128), F32),
                 pltpu.SemaphoreType.DMA((3,)),
                 pltpu.SemaphoreType.DMA((NR, 2)),
                 pltpu.SemaphoreType.DMA((NL, 2)),
                 pltpu.SemaphoreType.DMA((4,)),
-            ] + [pltpu.SemaphoreType.DMA((nsem,))] * 6 + [
+            ] + [pltpu.SemaphoreType.DMA((n,)) for n in (2, NA, 2, NB, NS, NX, 8)] + [
                 pltpu.SemaphoreType.DMA((3,)),
                 pltpu.SemaphoreType.DMA((3,)),
             ],
@@ -374,9 +410,9 @@
             out_specs=(hbm, hbm, hbm),
             scratch_shapes=[pltpu.VMEM((1, tokens), F32), pltpu.VMEM((1, tokens), F32),
                             pltpu.VMEM((tokens, vq), BF16),
-                            pltpu.SemaphoreType.DMA((pl.cdiv(vq, block),)), pltpu.SemaphoreType.DMA((2,))],
+                            pltpu.SemaphoreType.DMA((1,)), pltpu.SemaphoreType.DMA((2,))],
             compiler_params=pltpu.CompilerParams(vmem_limit_bytes=8 * 2 ** 20),
-        )(logits, stats, lncol)
+        )(exps, stats, scale)
         return log_norm.reshape(tokens), target_logprob.reshape(tokens), probs
 
     return jax.shard_map(local_scores, mesh=mesh,

time: 102 us -> 101 us (level)
  Pallas kernels: 101 us -> 99.1 us
    pallas_call x1, Pallas kernels: 99.5 us -> 97.7 us  [local_scores(): pl.pallas_call(functools.partial(scores_kernel, dims), out_shape=(pltpu.V...]
where the time goes in v4:
time: 101 us; the launch traced here: 100 us
  Pallas kernels  99.1 us (98%)
  between operations  1.29 us (1%)
    pallas_call x1, Pallas kernels, local_scores(): pl.pallas_call(functools.partial(scores_kernel, dims), out_shape=(pltpu.V...  97.7 us

profile of v4, /device:TPU:0, one launch (start us, length us, event | category | flops | bytes accessed | tf_op | source)
XLA Modules:
  0.0 100.4 jit_solution(2691651342097793781)
XLA Ops:
  1.3 97.7 %shard_map.76 = (f32[32,32128]{1,0:T(8,128)S(1)}, f32[8,128]{1,0:T(8,128)S(1)}, f32[32,128]{1,0:T(8,128)S(1)}) custom-call(f32[1,1]{1,0:T(1,128)} %bitcast.5.temp_ref, s32[1,32]{1,0:T(1,128)} %bitcast.7, bf16[32,3072]{1,0:T(8,128)(2,1)} %hid_hbm.1, bf16[24,128]{1,0:T(8,128)(2,1)} %bitcast.6, bf16[128256,768]{1,0:T(8,128)(2,1)} %table.1), custom_call_target="tpu_custom_call" | custom-call | tf_op jit(solution)/shard_map/pallas_call | solution.py:374
  99.0 1.4 %shard_map.77 = (f32[1,32]{1,0:T(1,128)}, f32[1,32]{1,0:T(1,128)}, bf16[32,32064]{1,0:T(8,128)(2,1)}) custom-call(f32[32,32128]{1,0:T(8,128)S(1)} %get-tuple-element.9.exp_ref, f32[8,128]{1,0:T(8,128)S(1)} %get-tuple-element.10.stats_ref, f32[32,128]{1,0:T(8,128)S(1)} %get-tuple-element.11.scale_ref), custom_call_target="tpu_custom_call" | custom-call | tf_op jit(solution)/shard_map/pallas_call | solution.py:404

commit v5 on v4

--- a/solution.py
+++ b/solution.py
@@ -13,7 +13,7 @@
 BF16 = jnp.bfloat16
 G = 4
 R = 256
-NR = 3
+NR = 2
 NL = 2
 LAG = 2
 LATE = 4
@@ -22,7 +22,7 @@
 
 def scores_kernel(dims, temp_ref, tgt_hbm, hid_hbm, gain_hbm, table, logits_ref, stats_ref, scale_ref,
                   tgt_ref, hid, gain, gain32, w, ring_r, ring_l, tail, ps, po, ls, lo, ra, rb, rx, rx2, acc, st,
-                  in_sem, r_sem, l_sem, tail_sem, as_sem, ar_sem, bs_sem, br_sem, xs_sem, xr_sem, one_sem, ss_sem, sr_sem):
+                  in_sem, r_sem, l_sem, as_sem, ar_sem, bs_sem, br_sem, xs_sem, xr_sem, one_sem, ss_sem, sr_sem):
     tokens, hidden_size, width, vq, nf, rt = dims
     me = lax.axis_index('tp')
     x = me // 2
@@ -47,7 +47,7 @@
 
     def tail_copy(i):
         start = pl.multiple_of(quarter((1 - x) if i < 2 else x, i % 2) + nf * rows, 64)
-        return pltpu.make_async_copy(table.at[pl.ds(start, trows)], tail.at[i], tail_sem.at[i])
+        return pltpu.make_async_copy(table.at[pl.ds(start, trows)], tail.at[i], (l_sem.at[0, i] if i < 2 else in_sem.at[i - 2]))
 
     def chunk(k):
         return pl.ds(pl.multiple_of(k * R, R), R)
@@ -341,14 +341,14 @@
     scale_ref[...] = jnp.broadcast_to(column(jnp.exp(own - log_norm)), (tokens, 128))
 
 
-def probs_kernel(block, vq, exp_ref, stats_ref, scale_ref, ln_hbm, tl_hbm, probs_hbm, ln, tl, probs, sem, small_sem):
+def probs_kernel(edges, exp_ref, stats_ref, scale_ref, ln_hbm, tl_hbm, probs_hbm, ln, tl, probs, sem, small_sem):
     tokens = ln.shape[1]
     ln[...] = stats_ref[0:1, :tokens]
     tl[...] = stats_ref[1:2, :tokens]
     copies = [pltpu.make_async_copy(ln, ln_hbm, small_sem.at[0]), pltpu.make_async_copy(tl, tl_hbm, small_sem.at[1])]
     scale = scale_ref[:, 0:1]
-    for i, start in enumerate(range(0, vq, block)):
-        sl = pl.ds(start, min(block, vq - start))
+    for i, (start, stop) in enumerate(zip(edges, edges[1:])):
+        sl = pl.ds(start, stop - start)
         probs[:, sl] = (exp_ref[:, sl] * scale).astype(BF16)
         if i == 0:
             for copy in copies:
@@ -392,7 +392,6 @@
                 pltpu.SemaphoreType.DMA((3,)),
                 pltpu.SemaphoreType.DMA((NR, 2)),
                 pltpu.SemaphoreType.DMA((NL, 2)),
-                pltpu.SemaphoreType.DMA((4,)),
             ] + [pltpu.SemaphoreType.DMA((n,)) for n in (2, NA, 2, NB, NS, NX, 8)] + [
                 pltpu.SemaphoreType.DMA((3,)),
                 pltpu.SemaphoreType.DMA((3,)),
@@ -400,9 +399,9 @@
             compiler_params=pltpu.CompilerParams(collective_id=0, has_side_effects=True,
                                                  vmem_limit_bytes=54 * 2 ** 20),
         )(temperature.reshape(1, 1), targets.reshape(1, tokens), hidden, final_gain.reshape(hidden_size // 128, 128), table)
-        block = 4096
+        edges = [0, 1024, 3072, 7168] + list(range(13312, vq - 4096, 6144)) + [vq]
         log_norm, target_logprob, probs = pl.pallas_call(
-            functools.partial(probs_kernel, block, vq),
+            functools.partial(probs_kernel, edges),
             out_shape=(jax.ShapeDtypeStruct((1, tokens), F32),
                        jax.ShapeDtypeStruct((1, tokens), F32),
                        jax.ShapeDtypeStruct((tokens, vq), BF16)),

time: 101 us -> 100 us (0.990)
  no operation moved by 1% of the time
where the time goes in v5:
time: 100 us
  Pallas kernels  99.1 us (99%)
  between operations  1.29 us (1%)
    pallas_call x1, Pallas kernels, local_scores(): pl.pallas_call(functools.partial(scores_kernel, dims), out_shape=(pltpu.V...  97.6 us

profile of v5, /device:TPU:0, one launch (start us, length us, event | category | flops | bytes accessed | tf_op | source)
XLA Modules:
  0.0 100.3 jit_solution(462915661269433813)
XLA Ops:
  1.3 97.6 %shard_map.76 = (f32[32,32128]{1,0:T(8,128)S(1)}, f32[8,128]{1,0:T(8,128)S(1)}, f32[32,128]{1,0:T(8,128)S(1)}) custom-call(f32[1,1]{1,0:T(1,128)} %bitcast.5.temp_ref, s32[1,32]{1,0:T(1,128)} %bitcast.7, bf16[32,3072]{1,0:T(8,128)(2,1)} %hid_hbm.1, bf16[24,128]{1,0:T(8,128)(2,1)} %bitcast.6, bf16[128256,768]{1,0:T(8,128)(2,1)} %table.1), custom_call_target="tpu_custom_call" | custom-call | tf_op jit(solution)/shard_map/pallas_call | solution.py:374
  98.9 1.4 %shard_map.77 = (f32[1,32]{1,0:T(1,128)}, f32[1,32]{1,0:T(1,128)}, bf16[32,32064]{1,0:T(8,128)(2,1)}) custom-call(f32[32,32128]{1,0:T(8,128)S(1)} %get-tuple-element.9.exp_ref, f32[8,128]{1,0:T(8,128)S(1)} %get-tuple-element.10.stats_ref, f32[32,128]{1,0:T(8,128)S(1)} %get-tuple-element.11.scale_ref), custom_call_target="tpu_custom_call" | custom-call | tf_op jit(solution)/shard_map/pallas_call | solution.py:403

commit v6 on v5

--- a/solution.py
+++ b/solution.py
@@ -22,7 +22,7 @@
 
 def scores_kernel(dims, temp_ref, tgt_hbm, hid_hbm, gain_hbm, table, logits_ref, stats_ref, scale_ref,
                   tgt_ref, hid, gain, gain32, w, ring_r, ring_l, tail, ps, po, ls, lo, ra, rb, rx, rx2, acc, st,
-                  in_sem, r_sem, l_sem, as_sem, ar_sem, bs_sem, br_sem, xs_sem, xr_sem, one_sem, ss_sem, sr_sem):
+                  in_sem, r_sem, l_sem, as_sem, ar_sem, bs_sem, br_sem, xs_sem, xr_sem, one_sem):
     tokens, hidden_size, width, vq, nf, rt = dims
     me = lax.axis_index('tp')
     x = me // 2
@@ -303,9 +303,10 @@
     for p in range(2):
         x_piece(p).wait_send()
     stat_copies = []
-    for i, peer in enumerate((xpeer, diag, sib)):
-        copy = pltpu.make_async_remote_copy(src_ref=st.at[me], dst_ref=st.at[me], send_sem=ss_sem.at[i],
-                                            recv_sem=sr_sem.at[i], device_id={'tp': peer}, device_id_type=MESH)
+    for peer, send, recv in ((xpeer, as_sem.at[0], one_sem.at[3]), (diag, as_sem.at[1], one_sem.at[5]),
+                             (sib, bs_sem.at[0], one_sem.at[1])):
+        copy = pltpu.make_async_remote_copy(src_ref=st.at[me], dst_ref=st.at[me], send_sem=send,
+                                            recv_sem=recv, device_id={'tp': peer}, device_id_type=MESH)
         copy.start()
         stat_copies.append(copy)
     pick = lax.broadcasted_iota(jnp.int32, (tokens, 128), 0) == lax.broadcasted_iota(jnp.int32, (tokens, 128), 1)
@@ -392,10 +393,7 @@
                 pltpu.SemaphoreType.DMA((3,)),
                 pltpu.SemaphoreType.DMA((NR, 2)),
                 pltpu.SemaphoreType.DMA((NL, 2)),
-            ] + [pltpu.SemaphoreType.DMA((n,)) for n in (2, NA, 2, NB, NS, NX, 8)] + [
-                pltpu.SemaphoreType.DMA((3,)),
-                pltpu.SemaphoreType.DMA((3,)),
-            ],
+            ] + [pltpu.SemaphoreType.DMA((n,)) for n in (2, NA, 2, NB, NS, NX, 8)],
             compiler_params=pltpu.CompilerParams(collective_id=0, has_side_effects=True,
                                                  vmem_limit_bytes=54 * 2 ** 20),
         )(temperature.reshape(1, 1), targets.reshape(1, tokens), hidden, final_gain.reshape(hidden_size // 128, 128), table)

time: 100 us -> 100 us (level)
  no operation moved by 1% of the time
where the time goes in v6:
time: 100 us
  Pallas kernels  99 us (99%)
  between operations  1.29 us (1%)
    pallas_call x1, Pallas kernels, local_scores(): pl.pallas_call(functools.partial(scores_kernel, dims), out_shape=(pltpu.V...  97.6 us

profile of v6, /device:TPU:0, one launch (start us, length us, event | category | flops | bytes accessed | tf_op | source)
XLA Modules:
  0.0 100.3 jit_solution(5626940036417364743)
XLA Ops:
  1.3 97.6 %shard_map.76 = (f32[32,32128]{1,0:T(8,128)S(1)}, f32[8,128]{1,0:T(8,128)S(1)}, f32[32,128]{1,0:T(8,128)S(1)}) custom-call(f32[1,1]{1,0:T(1,128)} %bitcast.5.temp_ref, s32[1,32]{1,0:T(1,128)} %bitcast.7, bf16[32,3072]{1,0:T(8,128)(2,1)} %hid_hbm.1, bf16[24,128]{1,0:T(8,128)(2,1)} %bitcast.6, bf16[128256,768]{1,0:T(8,128)(2,1)} %table.1), custom_call_target="tpu_custom_call" | custom-call | tf_op jit(solution)/shard_map/pallas_call | solution.py:375
  98.9 1.4 %shard_map.77 = (f32[1,32]{1,0:T(1,128)}, f32[1,32]{1,0:T(1,128)}, bf16[32,32064]{1,0:T(8,128)(2,1)}) custom-call(f32[32,32128]{1,0:T(8,128)S(1)} %get-tuple-element.9.exp_ref, f32[8,128]{1,0:T(8,128)S(1)} %get-tuple-element.10.stats_ref, f32[32,128]{1,0:T(8,128)S(1)} %get-tuple-element.11.scale_ref), custom_call_target="tpu_custom_call" | custom-call | tf_op jit(solution)/shard_map/pallas_call | solution.py:401

commit v7 on v6

--- a/solution.py
+++ b/solution.py
@@ -17,7 +17,7 @@
 NL = 2
 LAG = 2
 LATE = 4
-NA, NB, NS, NX = 5, 5, 5, 2 * LATE
+NA, NB, NS, NX = 4, 4, 5, 2 * LATE
 
 
 def scores_kernel(dims, temp_ref, tgt_hbm, hid_hbm, gain_hbm, table, logits_ref, stats_ref, scale_ref,

time: 100 us -> 100 us (level)
  no operation moved by 1% of the time
where the time goes in v7:
time: 100 us
  Pallas kernels  99 us (99%)
  between operations  1.29 us (1%)
    pallas_call x1, Pallas kernels, local_scores(): pl.pallas_call(functools.partial(scores_kernel, dims), out_shape=(pltpu.V...  97.6 us

profile of v7, /device:TPU:0, one launch (start us, length us, event | category | flops | bytes accessed | tf_op | source)
XLA Modules:
  0.0 100.3 jit_solution(8870066384907883329)
XLA Ops:
  1.3 97.6 %shard_map.76 = (f32[32,32128]{1,0:T(8,128)S(1)}, f32[8,128]{1,0:T(8,128)S(1)}, f32[32,128]{1,0:T(8,128)S(1)}) custom-call(f32[1,1]{1,0:T(1,128)} %bitcast.5.temp_ref, s32[1,32]{1,0:T(1,128)} %bitcast.7, bf16[32,3072]{1,0:T(8,128)(2,1)} %hid_hbm.1, bf16[24,128]{1,0:T(8,128)(2,1)} %bitcast.6, bf16[128256,768]{1,0:T(8,128)(2,1)} %table.1), custom_call_target="tpu_custom_call" | custom-call | tf_op jit(solution)/shard_map/pallas_call | solution.py:375
  98.9 1.4 %shard_map.77 = (f32[1,32]{1,0:T(1,128)}, f32[1,32]{1,0:T(1,128)}, bf16[32,32064]{1,0:T(8,128)(2,1)}) custom-call(f32[32,32128]{1,0:T(8,128)S(1)} %get-tuple-element.9.exp_ref, f32[8,128]{1,0:T(8,128)S(1)} %get-tuple-element.10.stats_ref, f32[32,128]{1,0:T(8,128)S(1)} %get-tuple-element.11.scale_ref), custom_call_target="tpu_custom_call" | custom-call | tf_op jit(solution)/shard_map/pallas_call | solution.py:401
